TPU v7x, 32 devices: a whole 2x2x4 slice. The times are simulated.
32 devices in a mesh: prow: 8 (over z, x), pcol: 4 (over y, core).
Axes of the slice: x: 2, y: 2, z: 4, core: 2. Of those that a mesh axis runs over, the one named last changes fastest.
Arguments:
- cross_cov: float32 [4, 8, 256, 8, 4, 256], P(None, 'prow', None, None, 'pcol'), may hold values from -6 to 6
- left_factor: float32 [4, 8, 256, 512], P(None, 'prow', None, 'pcol'), may hold values from -1 to 3, as said below
- right_factor: float32 [8, 4, 256, 512], P(None, 'pcol', None, 'prow'), may hold values from -1 to 3, as said below
Outputs:
- whitened: float32 [4, 8, 256, 8, 4, 256], P(None, 'prow', None, None, 'pcol')
Inputs may be any that keep to these rules, and one draw needn't show every extreme that they name: `left_factor`: the diagonal entries of the diagonal blocks lie between 1.5 and 2. `right_factor`: the diagonal entries of the diagonal blocks lie between 1.5 and 2.
All inputs are finite; a program needn't handle non-finite values.
Results may differ from a plain program's by a relative error of at most 0.0001.
Values sent between devices are 32-bit elements; how exact they have to be, the bound alone decides.
A program may use at most 128 MiB of HBM per device.

v0:
```python
import jax
import jax.numpy as jnp
from jax import lax
from jax.sharding import PartitionSpec as P

STEPS = 2


def spread(x, axis, root):
    mine = lax.axis_index(axis) == root
    return lax.psum(jnp.where(mine, x, jnp.zeros_like(x)), axis)


def solve_left(operands):
    diag_block, owned_rows = operands
    return jax.scipy.linalg.solve_triangular(diag_block, owned_rows, lower=True)


def solve_right(operands):
    diag_block, owned_cols = operands
    return jax.scipy.linalg.solve_triangular(diag_block, owned_cols.T, lower=True).T


def nothing_left(operands):
    return jnp.zeros_like(operands[1])


def shards(cross_cov, left_factor, right_factor):
    rows_axis = lax.axis_size("prow")
    cols_axis = lax.axis_size("pcol")
    my_row = lax.axis_index("prow")
    my_col = lax.axis_index("pcol")
    row_blocks = cross_cov.shape[0]
    block_size = cross_cov.shape[2]
    col_blocks = cross_cov.shape[3]
    left_rows = lax.all_gather(left_factor, "pcol", axis=3, tiled=True)[:, 0]
    right_rows = lax.all_gather(right_factor, "prow", axis=3, tiled=True)[:, 0]
    matrix = cross_cov.reshape(row_blocks, block_size, col_blocks * block_size)
    row_index = (jnp.arange(row_blocks) * rows_axis + my_row).reshape(row_blocks, 1, 1)

    def left_update(current, solved, block_step):
        first_col = block_step * block_size
        factor = left_rows[:, :, first_col : first_col + block_size]
        update = jnp.einsum("cij,jn->cin", factor, solved, precision=lax.Precision.HIGHEST)
        return jnp.where(
            row_index > block_step,
            current - update,
            jnp.where(row_index == block_step, solved[None], current),
        )

    for block_step in range(STEPS):
        local_block = block_step // rows_axis
        first_col = block_step * block_size
        diag_block = left_rows[local_block, :, first_col : first_col + block_size]
        solved = lax.cond(
            my_row == block_step % rows_axis,
            solve_left,
            nothing_left,
            (diag_block, matrix[local_block]),
        )
        solved = spread(solved, "prow", block_step % rows_axis)
        matrix = left_update(matrix, solved, block_step)
    columns = matrix.reshape(row_blocks * block_size, col_blocks, block_size)
    col_index = (jnp.arange(col_blocks) * cols_axis + my_col).reshape(1, col_blocks, 1)

    def right_update(current, solved, block_step):
        first_col = block_step * block_size
        factor = right_rows[:, :, first_col : first_col + block_size]
        update = jnp.einsum("rj,dsj->rds", solved, factor, precision=lax.Precision.HIGHEST)
        return jnp.where(
            col_index > block_step,
            current - update,
            jnp.where(col_index == block_step, solved[:, None, :], current),
        )

    for block_step in range(STEPS):
        local_block = block_step // cols_axis
        first_col = block_step * block_size
        diag_block = right_rows[local_block, :, first_col : first_col + block_size]
        solved = lax.cond(
            my_col == block_step % cols_axis,
            solve_right,
            nothing_left,
            (diag_block, columns[:, local_block]),
        )
        solved = spread(solved, "pcol", block_step % cols_axis)
        columns = right_update(columns, solved, block_step)
    return columns.reshape(cross_cov.shape)


def solution(mesh):
    placed = (
        P(None, "prow", None, None, "pcol", None),
        P(None, "prow", None, "pcol"),
        P(None, "pcol", None, "prow"),
    )
    return jax.shard_map(
        shards,
        mesh=mesh,
        in_specs=placed,
        out_specs=P(None, "prow", None, None, "pcol", None),
        check_vma=False,
    )
```

profile of v0, /device:TPU:0, one launch (start us, length us, event | category | flops | bytes accessed | tf_op | source)
XLA Modules:
  0.0 603.8 jit_solution(9120524464685021274)
XLA Ops:
  6.5 0.7 all-gather.3.cloned.1.call-update
  7.3 27.1 %all-gather.3.cloned.1.call-done = f32[4,1,256,512]{3,2,0,1:T(8,128)} async-done(((f32[4,1,256,128]{3,2,0,1:T(8,128)}), f32[4,1,256,512]{3,2,0,1:T(8,128)}) %all-gather.3.cloned.1.call-update) | async-done | bytes 2097168 | tf_op jit(solution)/shard_map/all_gather | solution.py:36
  34.5 34.7 %conditional.4 = (f32[256,2048]{0,1:T(8,128)}) conditional(s32[]{:T(128)} %convert_element_type.12, () %tuple.31, (f32[4,256,512]{2,1,0:T(8,128)}, f32[4,1,256,8,1,256]{5,4,3,2,1,0:T(1,128)}) %tuple.153), branch_computations={%region_0.0_spmd, %region_1.0_spmd} | conditional | flops 1208877056 | bytes 41746636 | solution.py:55
  34.5 3.9 copy.30
  38.5 0.9 copy.52
  39.4 1.0 bitcast_select_fusion
  40.5 3.9 while.8
  40.5 0.6 fusion.45
  41.1 1.3 bitcast_dynamic-update-slice_fusion.11
  42.4 0.6 fusion.45
  43.0 1.3 bitcast_dynamic-update-slice_fusion.11
  44.4 19.7 %custom-call.8 = f32[2,128,128]{1,2,0:T(8,128)S(1)} custom-call(f32[2,128,128]{2,1,0:T(8,128)S(1)} %get-tuple-element.87), custom_call_target="InvertDiagBlocksLowerTriangular" | custom-call | tf_op jit(solution)/shard_map/cond/branch_1_fun/jit(_solve_triangular)/triangular_solve | solution.py:16
  64.1 1.1 fusion
  65.1 1.0 convolution_subtract_fusion
  66.2 1.0 fusion.3
  67.4 1.8 copy.45
  69.2 3.1 broadcast_select_fusion.1
  72.5 20.6 %copy.28 = f32[4,1,256,8,1,256]{2,5,3,0,4,1:T(8,128)} copy(f32[4,1,256,8,1,256]{5,4,3,2,1,0:T(1,128)} %param.15) | data formatting | bytes 16777216 | tf_op args[0]
  93.2 77.7 %all-reduce.5.cloned.1.call-done = f32[256,2048]{0,1:T(8,128)} async-done(((f32[256,2048]{0,1:T(8,128)}), f32[256,2048]{0,1:T(8,128)}) %all-reduce.5.cloned.1.call-update) | async-done | bytes 2097168 | tf_op jit(solution)/shard_map/psum | solution.py:11
  170.9 13.9 %fusion.17 = f32[4,256,2048]{1,2,0:T(8,128)} fusion(f32[4,256,2048]{1,2,0:T(8,128)} %bitcast.129, f32[256,2048]{0,1:T(8,128)} %all-reduce.5.cloned.1.call-done, pred[4]{0:T(512)(128)(4,1)S(1)} %get-tuple-element.153, pred[4]{0:T(512)(128)(4,1)S(1)} %get-tuple-element.154, f32[4,256,512]{2,1,0:T(8,128)} %bitcast.139), kind=kOutput, calls=%fused_computation.58 | convolution fusion | flops 6448742400 | bytes 22020104 | tf_op jit(solution)/shard_map/cij,jn->cin/dot_general | solution.py:44
  184.8 1.4 conditional.5
  184.8 1.4 broadcast.151.clone
  186.2 1.5 broadcast_select_fusion
  187.8 1.1 copy.35
  189.2 139.5 %all-reduce.7.cloned.1.call-done = f32[256,2048]{0,1:T(8,128)} async-done(((f32[256,2048]{0,1:T(8,128)}), f32[256,2048]{0,1:T(8,128)}) %all-reduce.7.cloned.1.call-update) | async-done | bytes 2097168 | tf_op jit(solution)/shard_map/psum | solution.py:11
  328.7 14.2 %fusion.16 = f32[4,256,2048]{1,2,0:T(8,128)} fusion(f32[4,256,2048]{1,2,0:T(8,128)} %fusion.17, f32[256,2048]{0,1:T(8,128)} %all-reduce.7.cloned.1.call-done, pred[4]{0:T(512)(128)(4,1)S(1)} %get-tuple-element.155, pred[4]{0:T(512)(128)(4,1)S(1)} %get-tuple-element.156, f32[4,256,512]{2,1,0:T(8,128)S(1)} %bitcast.141), kind=kOutput, calls=%fused_computation.56 | convolution fusion | flops 6448742400 | bytes 22021120 | tf_op jit(solution)/shard_map/cij,jn->cin/dot_general | solution.py:44
  342.9 8.8 %copy.34 = f32[4,256,2048]{2,1,0:T(8,128)} copy(f32[4,256,2048]{1,2,0:T(8,128)} %fusion.16) | data formatting | bytes 16777216 | tf_op jit(solution)/shard_map/jit(_where)/select_n | solution.py:45
  351.7 10.9 %copy.53 = f32[128,8,8,256]{3,2,1,0:T(8,128)} copy(f32[128,8,8,256]{3,1,2,0:T(8,128)} %bitcast.130) | data formatting | bytes 16777216
  362.6 40.2 %all-gather.5.cloned.1.call-done = f32[8,1,256,512]{2,0,1,3:T(8,128)} async-done(((f32[8,1,256,64]{2,0,1,3:T(8,128)}), f32[8,1,256,512]{2,0,1,3:T(8,128)}) %all-gather.5.cloned.1.call-update) | async-done | bytes 4194320 | tf_op jit(solution)/shard_map/all_gather | solution.py:37
  402.8 5.3 copy.36
  408.1 37.0 %conditional.6 = (f32[1024,256]{1,0:T(8,128)S(1)}) conditional(s32[]{:T(128)} %convert_element_type.14, () %tuple.35, (f32[8,256,512]{2,1,0:T(8,128)}, f32[1024,8,256]{2,1,0:T(8,128)}) %tuple.151), branch_computations={%region_6.8_spmd, %region_7.10_spmd} | conditional | flops 604504064 | bytes 27590860 | solution.py:80
  408.5 8.7 %copy.37 = f32[1024,8,256]{0,2,1:T(8,128)} copy(f32[1024,8,256]{2,1,0:T(8,128)} %get-tuple-element.106) | data formatting | bytes 16777216 | tf_op jit(solution)/shard_map
  417.2 1.3 slice_bitcast_fusion.4
  418.5 1.0 bitcast_select_fusion.1
  419.6 3.6 while.10
  420.2 1.2 bitcast_dynamic-update-slice_fusion.9
  422.0 1.2 bitcast_dynamic-update-slice_fusion.9
  423.2 19.7 %custom-call.10 = f32[2,128,128]{1,2,0:T(8,128)S(1)} custom-call(f32[2,128,128]{2,1,0:T(8,128)S(1)} %get-tuple-element.89), custom_call_target="InvertDiagBlocksLowerTriangular" | custom-call | tf_op jit(solution)/shard_map/cond/branch_1_fun/jit(_solve_triangular)/triangular_solve | solution.py:21
  442.8 0.6 fusion.4
  443.5 0.6 convolution_subtract_fusion.1
  444.1 0.6 fusion.7
  445.2 1.1 broadcast_select_fusion.3
  446.3 34.0 %all-reduce.9.cloned.1.call-done = f32[1024,256]{1,0:T(8,128)} async-done(((f32[1024,256]{1,0:T(8,128)}), f32[1024,256]{1,0:T(8,128)}) %all-reduce.9.cloned.1.call-update) | async-done | bytes 1048592 | tf_op jit(solution)/shard_map/psum | solution.py:11
  480.4 17.0 %select_select_fusion.1 = f32[1024,8,256]{2,0,1:T(8,128)} fusion(f32[1024,8,256]{2,1,0:T(8,128)} %bitcast.127, f32[1024,256]{1,0:T(8,128)} %all-reduce.9.cloned.1.call-done, pred[8]{0:T(512)(128)(4,1)S(1)} %get-tuple-element.157, pred[8]{0:T(512)(128)(4,1)S(1)} %get-tuple-element.158, f32[8,256,512]{2,1,0:T(8,128)} %bitcast.132), kind=kOutput, calls=%fused_computation.60 | convolution fusion | flops 6448742400 | bytes 20971536 | tf_op jit(solution)/shard_map/rj,dsj->rds/dot_general | solution.py:69
  497.6 1.0 broadcast_select_fusion.2
  498.7 72.5 %all-reduce.11.cloned.1.call-done = f32[1024,256]{1,0:T(8,128)} async-done(((f32[1024,256]{1,0:T(8,128)}), f32[1024,256]{1,0:T(8,128)}) %all-reduce.11.cloned.1.call-update) | async-done | bytes 1048592 | tf_op jit(solution)/shard_map/psum | solution.py:11
  571.2 12.9 %select_select_fusion = f32[1024,8,256]{2,0,1:T(8,128)S(1)} fusion(f32[1024,8,256]{2,0,1:T(8,128)} %select_select_fusion.1, f32[1024,256]{1,0:T(8,128)} %all-reduce.11.cloned.1.call-done, pred[8]{0:T(512)(128)(4,1)S(1)} %get-tuple-element.159, pred[8]{0:T(512)(128)(4,1)S(1)} %get-tuple-element.160, f32[8,256,512]{2,1,0:T(8,128)} %bitcast.134), kind=kOutput, calls=%fused_computation.59 | convolution fusion | flops 6448742400 | bytes 20971536 | tf_op jit(solution)/shard_map/rj,dsj->rds/dot_general | solution.py:69
  584.1 12.7 %copy.43 = f32[4,1,256,8,1,256]{5,4,3,2,1,0:T(1,128)} copy(f32[4,1,256,8,1,256]{5,2,0,3,4,1:T(8,128)S(1)} %bitcast.128) | data formatting | bytes 16777216 | tf_op jit(solution)/shard_map/reshape | solution.py:88
  (37 shorter events, 3.1 us)
Async XLA Ops:
  6.5 27.9 %all-gather.3.cloned.1.call-start = ((), (), s32[]{:S(2)}) async-start(), calls=%async_computation | async-start | bytes 2621440 | tf_op jit(solution)/shard_map/all_gather | solution.py:36
  7.3 163.6 %all-reduce.5.cloned.1.call-start = ((), (), s32[]{:S(2)}) async-start(), calls=%async_computation.1 | async-start | bytes 4194304 | tf_op jit(solution)/shard_map/psum | solution.py:11
  72.3 256.5 %all-reduce.7.cloned.1.call-start = ((), (), s32[]{:S(2)}) async-start(), calls=%async_computation.2 | async-start | bytes 4194304 | tf_op jit(solution)/shard_map/psum | solution.py:11
  186.2 1.6 copy-start.1
  187.7 141.0 %copy-start = (f32[4,1,256,512]{3,2,0,1:T(8,128)S(1)}, f32[4,1,256,512]{3,2,0,1:T(8,128)}, u32[]{:S(2)}) copy-start(f32[4,1,256,512]{3,2,0,1:T(8,128)} %all-gather.3.cloned.1.call-done) | copy-start | bytes 6291460
  187.7 215.1 %all-gather.5.cloned.1.call-start = ((), (), s32[]{:S(2)}) async-start(), calls=%async_computation.3 | async-start | bytes 4718592 | tf_op jit(solution)/shard_map/all_gather | solution.py:37
  188.9 291.4 %all-reduce.9.cloned.1.call-start = ((), (), s32[]{:S(2)}) async-start(), calls=%async_computation.4 | async-start | bytes 2097152 | tf_op jit(solution)/shard_map/psum | solution.py:11
  446.3 124.9 %all-reduce.11.cloned.1.call-start = ((), (), s32[]{:S(2)}) async-start(), calls=%async_computation.5 | async-start | bytes 2097152 | tf_op jit(solution)/shard_map/psum | solution.py:11
Sparse Core Ops, SparseCore 0:
  8.9 25.5 all-gather.2
  72.4 98.4 all-reduce.4
  187.8 140.8 all-reduce.6
  330.7 72.0 all-gather.4
  446.4 33.9 all-reduce.8
  498.8 72.3 all-reduce.10
where the time goes:
time: 611 us; the launch traced here: 604 us
  waiting for transfers between devices  392 us (64%)
  local copies, waits for them, and re-layouts  85.6 us (14%)
  matrix products  62.9 us (10%)
  other arithmetic  48.3 us (8%)
  between operations  13.7 us (2%)
    psum x4, waiting for transfers between devices, spread(): return lax.psum(jnp.where(mine, x, jnp.zeros_like(x)), axis)  324 us
    all_gather x1, waiting for transfers between devices, shards(): right_rows = lax.all_gather(right_factor, 'prow', axis=3, tiled=True)[:, 0]  40.2 us
    unnamed x7, local copies, waits for them, and re-layouts  32.7 us
    dot_general x2, matrix products, right_update(): jnp.einsum('rj,dsj->rds', solved, factor, precision=lax.Precision.HIGHEST)  29.9 us
    dot_general x2, matrix products, left_update(): jnp.einsum('cij,jn->cin', factor, solved, precision=lax.Precision.HIGHEST)  28.1 us
    all_gather x1, waiting for transfers between devices, shards(): left_rows = lax.all_gather(left_factor, 'pcol', axis=3, tiled=True)[:, 0]  27.1 us
    another operation x5, other arithmetic, solve_left(): return jax.scipy.linalg.solve_triangular(diag_block, owned_rows, lower=True)  20.8 us
    another operation x4, other arithmetic, solve_right(): jax.scipy.linalg.solve_triangular(diag_block, owned_cols.T, lower=True)  20.6 us
  transfers between devices with their start and end apart: 6, of which 6 were waited for; matrix products, arithmetic and copies ran while one was open for 9% of the time, Pallas kernels for 0%

commit v1 on v0

--- a/solution.py
+++ b/solution.py
@@ -8,7 +8,7 @@
 
 def spread(x, axis, root):
     mine = lax.axis_index(axis) == root
-    return lax.psum(jnp.where(mine, x, jnp.zeros_like(x)), axis)
+    return jnp.sum(lax.all_gather(jnp.where(mine, x, jnp.zeros_like(x)), axis), axis=0)
 
 
 def solve_left(operands):

time: 611 us -> 880 us (1.44)
  waiting for transfers between devices: 392 us -> 593 us
  matrix products: 62.9 us -> 89 us
  other arithmetic: 48.3 us -> 74.3 us
  local copies, waits for them, and re-layouts: 85.6 us -> 101 us
    all_gather x0 -> x4, waiting for transfers between devices: none -> 526 us  [spread(): lax.all_gather(jnp.where(mine, x, jnp.zeros_like(x)), axis)]
    psum x4 -> x0, waiting for transfers between devices: 324 us -> none  [spread(): return lax.psum(jnp.where(mine, x, jnp.zeros_like(x)), axis)]
    reduce_sum x0 -> x4, other arithmetic: none -> 27.7 us  [spread(): jnp.sum(lax.all_gather(jnp.where(mine, x, jnp.zeros_like(x)), axis), axis=0)]
    dot_general x2, matrix products: 28.1 us -> 41.8 us  [left_update(): jnp.einsum('cij,jn->cin', factor, solved, precision=lax.Precision.HIGHEST)]
    dot_general x2, matrix products: 29.9 us -> 42.2 us  [right_update(): jnp.einsum('rj,dsj->rds', solved, factor, precision=lax.Precision.HIGHEST)]
    all_gather x0 -> x2, local copies, waits for them, and re-layouts: none -> 12.1 us  [spread(): lax.all_gather(jnp.where(mine, x, jnp.zeros_like(x)), axis)]
    unnamed x7 -> x5, local copies, waits for them, and re-layouts: 32.7 us -> 33.8 us
  transfers between devices with their start and end apart: 6 -> 6, of which waited for: 6 -> 6; matrix products, arithmetic and copies ran while one was open for 9% -> 7% of each run, Pallas kernels for 0% -> 0%
where the time goes in v1:
time: 880 us; the launch traced here: 873 us
  waiting for transfers between devices  593 us (67%)
  local copies, waits for them, and re-layouts  101 us (11%)
  matrix products  89 us (10%)
  other arithmetic  74.3 us (8%)
  between operations  13.8 us (2%)
    all_gather x4, waiting for transfers between devices, spread(): lax.all_gather(jnp.where(mine, x, jnp.zeros_like(x)), axis)  526 us
    dot_general x2, matrix products, right_update(): jnp.einsum('rj,dsj->rds', solved, factor, precision=lax.Precision.HIGHEST)  42.2 us
    dot_general x2, matrix products, left_update(): jnp.einsum('cij,jn->cin', factor, solved, precision=lax.Precision.HIGHEST)  41.8 us
    all_gather x1, waiting for transfers between devices, shards(): right_rows = lax.all_gather(right_factor, 'prow', axis=3, tiled=True)[:, 0]  39 us
    unnamed x5, local copies, waits for them, and re-layouts  33.8 us
    reduce_sum x4, other arithmetic, spread(): jnp.sum(lax.all_gather(jnp.where(mine, x, jnp.zeros_like(x)), axis), axis=0)  27.7 us
    all_gather x1, waiting for transfers between devices, shards(): left_rows = lax.all_gather(left_factor, 'pcol', axis=3, tiled=True)[:, 0]  27.1 us
    another operation x5, other arithmetic, solve_left(): return jax.scipy.linalg.solve_triangular(diag_block, owned_rows, lower=True)  20.8 us
  transfers between devices with their start and end apart: 6, of which 6 were waited for; matrix products, arithmetic and copies ran while one was open for 7% of the time, Pallas kernels for 0%

profile of v1, /device:TPU:0, one launch (start us, length us, event | category | flops | bytes accessed | tf_op | source)
XLA Modules:
  0.0 872.5 jit_solution(8404068294229076128)
XLA Ops:
  7.3 27.1 %all-gather.11.cloned.1.call-done = f32[4,1,256,512]{3,2,0,1:T(8,128)} async-done(((f32[4,1,256,128]{3,2,0,1:T(8,128)}), f32[4,1,256,512]{3,2,0,1:T(8,128)}) %all-gather.11.cloned.1.call-update) | async-done | bytes 2097168 | tf_op jit(solution)/shard_map/all_gather | solution.py:36
  34.5 33.2 %conditional.4 = (f32[256,2048]{1,0:T(8,128)S(1)}) conditional(s32[]{:T(128)} %convert_element_type.12, () %tuple.31, (f32[4,256,512]{2,1,0:T(8,128)}, f32[4,1,256,8,1,256]{5,4,3,2,1,0:T(1,128)}) %tuple.145), branch_computations={%region_0.0_spmd, %region_1.0_spmd} | conditional | flops 1208877056 | bytes 37552324 | solution.py:55
  34.5 1.0 bitcast_select_fusion
  35.5 4.2 while.8
  36.2 1.5 bitcast_dynamic-update-slice_fusion.11
  38.3 1.5 bitcast_dynamic-update-slice_fusion.11
  39.8 19.7 %custom-call.8 = f32[2,128,128]{1,2,0:T(8,128)S(1)} custom-call(f32[2,128,128]{2,1,0:T(8,128)S(1)} %get-tuple-element.87), custom_call_target="InvertDiagBlocksLowerTriangular" | custom-call | tf_op jit(solution)/shard_map/cond/branch_1_fun/jit(_solve_triangular)/triangular_solve | solution.py:16
  59.5 3.9 copy.22
  63.5 0.9 copy.48
  64.4 1.0 fusion
  65.5 1.0 convolution_subtract_fusion
  66.5 1.1 fusion.3
  67.7 1.5 broadcast_select_fusion.1
  69.3 1.0 copy-done
  70.2 1.1 copy.29
  71.6 20.9 %copy.20 = f32[4,1,256,8,1,256]{2,5,3,0,4,1:T(8,128)} copy(f32[4,1,256,8,1,256]{5,4,3,2,1,0:T(1,128)} %param.15) | data formatting | bytes 16777216 | tf_op args[0]
  92.5 200.3 %all-gather.15.cloned.1.call-done = f32[2048,2048]{1,0:T(8,128)} async-done(((f32[256,2048]{1,0:T(8,128)}), f32[2048,2048]{1,0:T(8,128)}) %all-gather.15.cloned.1.call-update) | async-done | bytes 16777232 | tf_op jit(solution)/shard_map/all_gather | solution.py:11
  292.8 9.1 %reduce_sum.36 = f32[256,2048]{1,0:T(8,128)} reduce(f32[8,256,2048]{2,1,0:T(8,128)} %bitcast.142, f32[]{:T(128)} %constant.48.clone.1), dimensions={0}, to_apply=%region_2.4 | reduce | flops 3670016 | bytes 18874372 | tf_op jit(solution)/shard_map/reduce_sum | solution.py:11
  301.9 2.0 copy.24
  303.8 20.9 %fusion.17 = f32[4,256,2048]{1,2,0:T(8,128)} fusion(f32[4,256,2048]{1,2,0:T(8,128)} %bitcast.134, f32[256,2048]{0,1:T(8,128)S(1)} %copy.24, pred[4]{0:T(512)(128)(4,1)S(1)} %get-tuple-element.149, pred[4]{0:T(512)(128)(4,1)S(1)} %get-tuple-element.150, f32[256,2048]{1,0:T(8,128)} %reduce_sum.36, f32[4,256,512]{2,1,0:T(8,128)} %bitcast.147), kind=kOutput, calls=%fused_computation.58 | convolution fusion | flops 6448742400 | bytes 22020104 | tf_op jit(solution)/shard_map/cij,jn->cin/dot_general | solution.py:44
  325.4 1.5 broadcast_select_fusion
  326.9 39.0 %all-gather.13.cloned.1.call-done = f32[8,1,256,512]{2,0,1,3:T(8,128)} async-done(((f32[8,1,256,64]{2,0,1,3:T(8,128)}), f32[8,1,256,512]{2,0,1,3:T(8,128)}) %all-gather.13.cloned.1.call-update) | async-done | bytes 4194320 | tf_op jit(solution)/shard_map/all_gather | solution.py:37
  365.9 5.3 copy.30
  371.2 222.6 %all-gather.17.cloned.1.call-done = f32[2048,2048]{1,0:T(8,128)} async-done(((f32[256,2048]{1,0:T(8,128)}), f32[2048,2048]{1,0:T(8,128)}) %all-gather.17.cloned.1.call-update) | async-done | bytes 16777232 | tf_op jit(solution)/shard_map/all_gather | solution.py:11
  593.7 9.1 %reduce_sum.37 = f32[256,2048]{1,0:T(8,128)} reduce(f32[8,256,2048]{2,1,0:T(8,128)} %bitcast.141, f32[]{:T(128)} %constant.48.clone.1), dimensions={0}, to_apply=%region_5.7 | reduce | flops 3670016 | bytes 18874372 | tf_op jit(solution)/shard_map/reduce_sum | solution.py:11
  602.9 1.9 copy.27
  604.8 20.9 %fusion.16 = f32[4,256,2048]{1,2,0:T(8,128)} fusion(f32[4,256,2048]{1,2,0:T(8,128)} %fusion.17, f32[256,2048]{0,1:T(8,128)S(1)} %copy.27, pred[4]{0:T(512)(128)(4,1)S(1)} %get-tuple-element.151, pred[4]{0:T(512)(128)(4,1)S(1)} %get-tuple-element.152, f32[256,2048]{1,0:T(8,128)} %reduce_sum.37, f32[4,256,512]{2,1,0:T(8,128)} %bitcast.149), kind=kOutput, calls=%fused_computation.56 | convolution fusion | flops 6448742400 | bytes 22020104 | tf_op jit(solution)/shard_map/cij,jn->cin/dot_general | solution.py:44
  625.7 9.0 %copy.28 = f32[4,256,2048]{2,1,0:T(8,128)} copy(f32[4,256,2048]{1,2,0:T(8,128)} %fusion.16) | data formatting | bytes 16777216 | tf_op jit(solution)/shard_map/jit(_where)/select_n | solution.py:45
  634.6 10.9 %copy.49 = f32[128,8,8,256]{3,2,1,0:T(8,128)} copy(f32[128,8,8,256]{3,1,2,0:T(8,128)} %bitcast.136) | data formatting | bytes 16777216
  645.5 36.7 %conditional.6 = (f32[1024,256]{0,1:T(8,128)S(1)}) conditional(s32[]{:T(128)} %convert_element_type.14, () %tuple.35, (f32[8,256,512]{2,1,0:T(8,128)}, f32[1024,8,256]{2,1,0:T(8,128)}) %tuple.143), branch_computations={%region_6.8_spmd, %region_7.10_spmd} | conditional | flops 604504064 | bytes 25493700 | solution.py:80
  645.5 1.0 bitcast_select_fusion.1
  646.6 3.9 while.10
  647.2 1.3 bitcast_dynamic-update-slice_fusion.9
  649.1 1.3 bitcast_dynamic-update-slice_fusion.9
  650.5 19.7 %custom-call.10 = f32[2,128,128]{1,2,0:T(8,128)S(1)} custom-call(f32[2,128,128]{2,1,0:T(8,128)S(1)} %get-tuple-element.89), custom_call_target="InvertDiagBlocksLowerTriangular" | custom-call | tf_op jit(solution)/shard_map/cond/branch_1_fun/jit(_solve_triangular)/triangular_solve | solution.py:21
  670.2 8.8 %copy.31 = f32[1024,8,256]{0,2,1:T(8,128)} copy(f32[1024,8,256]{2,1,0:T(8,128)} %get-tuple-element.106) | data formatting | bytes 16777216 | tf_op jit(solution)/shard_map
  678.9 1.3 slice_bitcast_fusion.4
  682.3 1.1 broadcast_select_fusion.3
  683.4 31.8 %all-gather.19.cloned.1.call-done = f32[4096,256]{0,1:T(8,128)} async-done(((f32[1024,256]{0,1:T(8,128)}), f32[4096,256]{0,1:T(8,128)}) %all-gather.19.cloned.1.call-update) | async-done | bytes 4194320 | tf_op jit(solution)/shard_map/all_gather | solution.py:11
  715.2 6.1 reshape.112
  721.4 4.7 reduce_sum.38
  726.4 24.3 %select_select_fusion.1 = f32[1024,8,256]{2,0,1:T(8,128)} fusion(f32[1024,8,256]{2,1,0:T(8,128)} %bitcast.133, f32[1024,256]{1,0:T(8,128)S(1)} %copy.34, pred[8]{0:T(512)(128)(4,1)S(1)} %get-tuple-element.153, pred[8]{0:T(512)(128)(4,1)S(1)} %get-tuple-element.154, f32[8,256,512]{2,1,0:T(8,128)} %bitcast.138, f32[1024,256]{0,1:T(8,128)S(1)} %reduce_sum.38), kind=kOutput, calls=%fused_computation.60 | convolution fusion | flops 6448742400 | bytes 20971536 | tf_op jit(solution)/shard_map/rj,dsj->rds/dot_general | solution.py:69
  751.1 1.0 broadcast_select_fusion.2
  752.2 71.7 %all-gather.21.cloned.1.call-done = f32[4096,256]{0,1:T(8,128)} async-done(((f32[1024,256]{0,1:T(8,128)}), f32[4096,256]{0,1:T(8,128)}) %all-gather.21.cloned.1.call-update) | async-done | bytes 4194320 | tf_op jit(solution)/shard_map/all_gather | solution.py:11
  823.8 6.0 reshape.113
  829.8 4.7 reduce_sum.39
  834.9 17.9 %select_select_fusion = f32[1024,8,256]{2,0,1:T(8,128)S(1)} fusion(f32[1024,8,256]{2,0,1:T(8,128)} %select_select_fusion.1, f32[1024,256]{1,0:T(8,128)S(1)} %copy.38, pred[8]{0:T(512)(128)(4,1)S(1)} %get-tuple-element.155, pred[8]{0:T(512)(128)(4,1)S(1)} %get-tuple-element.156, f32[8,256,512]{2,1,0:T(8,128)} %bitcast.140, f32[1024,256]{0,1:T(8,128)S(1)} %reduce_sum.39), kind=kOutput, calls=%fused_computation.59 | convolution fusion | flops 6448742400 | bytes 20971536 | tf_op jit(solution)/shard_map/rj,dsj->rds/dot_general | solution.py:69
  852.8 12.7 %copy.39 = f32[4,1,256,8,1,256]{5,4,3,2,1,0:T(1,128)} copy(f32[4,1,256,8,1,256]{5,2,0,3,4,1:T(8,128)S(1)} %bitcast.135) | data formatting | bytes 16777216 | tf_op jit(solution)/shard_map/reshape | solution.py:88
  (43 shorter events, 8.0 us)
Async XLA Ops:
  6.5 27.9 %all-gather.11.cloned.1.call-start = ((), (), s32[]{:S(2)}) async-start(), calls=%async_computation | async-start | bytes 2621440 | tf_op jit(solution)/shard_map/all_gather | solution.py:36
  7.3 285.5 %all-gather.15.cloned.1.call-start = ((), (), s32[]{:S(2)}) async-start(), calls=%async_computation.2 | async-start | bytes 18874368 | tf_op jit(solution)/shard_map/all_gather | solution.py:11
  69.2 1.0 copy-start
  69.2 296.7 %all-gather.13.cloned.1.call-start = ((), (), s32[]{:S(2)}) async-start(), calls=%async_computation.1 | async-start | bytes 4718592 | tf_op jit(solution)/shard_map/all_gather | solution.py:37
  71.4 522.4 %all-gather.17.cloned.1.call-start = ((), (), s32[]{:S(2)}) async-start(), calls=%async_computation.3 | async-start | bytes 18874368 | tf_op jit(solution)/shard_map/all_gather | solution.py:11
  326.9 388.4 %all-gather.19.cloned.1.call-start = ((), (), s32[]{:S(2)}) async-start(), calls=%async_computation.4 | async-start | bytes 5242880 | tf_op jit(solution)/shard_map/all_gather | solution.py:11
  683.4 140.5 %all-gather.21.cloned.1.call-start = ((), (), s32[]{:S(2)}) async-start(), calls=%async_computation.5 | async-start | bytes 5242880 | tf_op jit(solution)/shard_map/all_gather | solution.py:11
Sparse Core Ops, SparseCore 0:
  8.9 25.5 all-gather.10
  69.3 223.3 all-gather.14
  294.9 70.9 all-gather.12
  367.9 225.7 all-gather.16
  683.5 31.7 all-gather.18
  752.3 71.5 all-gather.20
